TPU v7x, 32 devices: a whole 2x2x4 slice. The times are simulated.
32 devices in a mesh: row: 8 (over y, x, core), col: 4 (over z).
Axes of the slice: x: 2, y: 2, z: 4, core: 2. Of those that a mesh axis runs over, the one named last changes fastest.
Arguments:
- weights: int32 [4096, 4096], P('row', 'col'), may hold values from 1 to 64
Outputs:
- distances: int32 [4096, 4096], P('row', 'col')
All inputs are finite; a program needn't handle non-finite values.
Results may differ from a plain program's by a relative error of at most 0.000001.
Values may be sent and summed in bfloat16 or wider, within the bound.
A program may use at most 64 MiB of HBM per device.

v0:
```python
import jax
import jax.numpy as jnp
from jax import lax
from jax.sharding import PartitionSpec as P

PIVOT = 128
STEPS = 4


def broadcast(value, axis, source):
    kept = jnp.where(lax.axis_index(axis) == source, value, 0).astype(value.dtype)
    return lax.psum(kept, axis)


def min_plus(acc, left, right):
    group = 8
    count = left.shape[1] // group

    def update(index, total):
        begin = (index * group).astype(jnp.int32)
        left_part = lax.dynamic_slice_in_dim(left, begin, group, 1)
        right_part = lax.dynamic_slice_in_dim(right, begin, group, 0)
        return jnp.minimum(total, jnp.min(left_part[:, :, None] + right_part[None, :, :], axis=1))

    return lax.fori_loop(0, count, update, acc)


def close_block(block):

    def relax(vertex, current):
        vertex = jnp.asarray(vertex).astype(jnp.int32)
        column = lax.dynamic_slice_in_dim(current, vertex, 1, 1)
        across = lax.dynamic_slice_in_dim(current, vertex, 1, 0)
        return jnp.minimum(current, column + across)

    return lax.fori_loop(0, block.shape[0], relax, block)


def per_device(weights):
    rows_dev, cols_dev = weights.shape
    verts = rows_dev * lax.axis_size("row")
    stride = verts // STEPS
    row_ids = lax.axis_index("row") * rows_dev + jnp.arange(rows_dev, dtype=jnp.int32)
    col_ids = lax.axis_index("col") * cols_dev + jnp.arange(cols_dev, dtype=jnp.int32)
    dist = jnp.where(row_ids[:, None] == col_ids[None, :], jnp.int32(0), weights).astype(jnp.int32)
    for step in range(STEPS):
        first = step * stride
        row_root = first // rows_dev
        row_off = first - row_root * rows_dev
        col_root = first // cols_dev
        col_off = first - col_root * cols_dev
        strip_rows = dist[row_off : row_off + PIVOT, :]
        strip_cols = dist[:, col_off : col_off + PIVOT]
        panel_rows = jax.tree.map(lambda part: broadcast(part, "row", row_root), strip_rows)
        closed = close_block(panel_rows[:, col_off : col_off + PIVOT])
        new_cols = min_plus(strip_cols, strip_cols, closed)
        panel_cols = jax.tree.map(lambda part: broadcast(part, "col", col_root), new_cols)
        dist = min_plus(dist, panel_cols, panel_rows)
    return dist


def solution(mesh):
    placed = (P("row", "col"),)
    return jax.shard_map(
        per_device, mesh=mesh, in_specs=placed, out_specs=P("row", "col"), check_vma=False
    )
```

profile of v0, /device:TPU:0, one launch (start us, length us, event | category | flops | bytes accessed | tf_op | source)
XLA Modules:
  0.0 1356.6 jit_solution(568644067238902018)
XLA Ops:
  9.3 58.6 %all-reduce.9.cloned.1.call-done = s32[128,1024]{1,0:T(8,128)} async-done(((s32[128,1024]{1,0:T(8,128)}), s32[128,1024]{1,0:T(8,128)}) %all-reduce.9.cloned.1.call-update) | async-done | bytes 524304 | tf_op jit(solution)/shard_map/psum | solution.py:12
  68.8 40.3 %while.156 = (s32[]{:T(128)}, s32[128,128]{1,0:T(8,128)S(1)}, s32[]{:T(128)}) while((s32[]{:T(128)}, s32[128,128]{1,0:T(8,128)S(1)}, s32[]{:T(128)}) %tuple.281), condition=%wide.region_2.3_spmd, body=%wide.region_1.2_spmd.sunk | while | flops 32770 | bytes 134197 | solution.py:36
  109.2 50.6 %while.157 = (s32[]{:T(128)}, s32[512,128]{1,0:T(8,128)S(1)}, s32[512,128]{1,0:T(8,128)S(1)}, s32[128,128]{1,0:T(8,128)S(1)}, s32[]{:T(128)}, /*index=5*/s32[]{:T(128)}, s32[]{:T(128)}, s32[]{:T(128)}) while((s32[]{:T(128)}, s32[512,128]{1,0:T(8,128)S(1)}, s32[512,128]{1,0:T(8,128)S(1)}, s32[128,128]{1,0:T(8,128)S(1)}, s32[]{:T(128)}, ...), condition=%wide.region_5.6_spmd, body=%wide.region_3.5_spmd.sunk | while | flops 1048582 | bytes 1110155 | solution.py:25
  160.6 34.8 %all-reduce.11.cloned.1.call-done = s32[512,128]{1,0:T(8,128)} async-done(((s32[512,128]{1,0:T(8,128)}), s32[512,128]{1,0:T(8,128)}) %all-reduce.11.cloned.1.call-update) | async-done | bytes 262160 | tf_op jit(solution)/shard_map/psum | solution.py:12
  195.4 150.9 %while.158 = (s32[]{:T(128)}, s32[512,1024]{1,0:T(8,128)S(1)}, s32[512,128]{1,0:T(8,128)}, s32[128,1024]{1,0:T(8,128)}, s32[]{:T(128)}, /*index=5*/s32[]{:T(128)}, s32[]{:T(128)}, s32[]{:T(128)}) while((s32[]{:T(128)}, s32[512,1024]{1,0:T(8,128)S(1)}, s32[512,128]{1,0:T(8,128)}, s32[128,1024]{1,0:T(8,128)}, s32[]{:T(128)}, ...), condition=%wide.region_9.10_spmd, body=%wide.region_7.9_spmd.sunk | while | flops 8388614 | bytes 8536203 | solution.py:25
  329.3 6.9 add_reduce_fusion.17
  338.7 6.9 add_reduce_fusion.17
  347.3 54.7 %all-reduce.13.cloned.1.call-done = s32[128,1024]{1,0:T(8,128)} async-done(((s32[128,1024]{1,0:T(8,128)}), s32[128,1024]{1,0:T(8,128)}) %all-reduce.13.cloned.1.call-update) | async-done | bytes 524304 | tf_op jit(solution)/shard_map/psum | solution.py:12
  402.9 40.3 %while.159 = (s32[]{:T(128)}, s32[128,128]{1,0:T(8,128)S(1)}, s32[]{:T(128)}) while((s32[]{:T(128)}, s32[128,128]{1,0:T(8,128)S(1)}, s32[]{:T(128)}) %tuple.290), condition=%wide.region_12.13_spmd, body=%wide.region_11.12_spmd.sunk | while | flops 32770 | bytes 134197 | solution.py:36
  443.2 50.6 %while.160 = (s32[]{:T(128)}, s32[512,128]{1,0:T(8,128)S(1)}, s32[512,128]{1,0:T(8,128)S(1)}, s32[128,128]{1,0:T(8,128)S(1)}, s32[]{:T(128)}, /*index=5*/s32[]{:T(128)}, s32[]{:T(128)}, s32[]{:T(128)}) while((s32[]{:T(128)}, s32[512,128]{1,0:T(8,128)S(1)}, s32[512,128]{1,0:T(8,128)S(1)}, s32[128,128]{1,0:T(8,128)S(1)}, s32[]{:T(128)}, ...), condition=%wide.region_15.16_spmd, body=%wide.region_13.15_spmd.sunk | while | flops 1048582 | bytes 1110155 | solution.py:25
  494.6 34.8 %all-reduce.15.cloned.1.call-done = s32[512,128]{1,0:T(8,128)} async-done(((s32[512,128]{1,0:T(8,128)}), s32[512,128]{1,0:T(8,128)}) %all-reduce.15.cloned.1.call-update) | async-done | bytes 262160 | tf_op jit(solution)/shard_map/psum | solution.py:12
  529.5 150.9 %while.161 = (s32[]{:T(128)}, s32[512,1024]{1,0:T(8,128)S(1)}, s32[512,128]{1,0:T(8,128)}, s32[128,1024]{1,0:T(8,128)}, s32[]{:T(128)}, /*index=5*/s32[]{:T(128)}, s32[]{:T(128)}, s32[]{:T(128)}) while((s32[]{:T(128)}, s32[512,1024]{1,0:T(8,128)S(1)}, s32[512,128]{1,0:T(8,128)}, s32[128,1024]{1,0:T(8,128)}, s32[]{:T(128)}, ...), condition=%wide.region_19.20_spmd, body=%wide.region_17.19_spmd.sunk | while | flops 8388614 | bytes 8536203 | solution.py:25
  559.6 6.9 add_reduce_fusion.19
  569.0 6.9 add_reduce_fusion.19
  681.3 54.7 %all-reduce.17.cloned.1.call-done = s32[128,1024]{1,0:T(8,128)} async-done(((s32[128,1024]{1,0:T(8,128)}), s32[128,1024]{1,0:T(8,128)}) %all-reduce.17.cloned.1.call-update) | async-done | bytes 524304 | tf_op jit(solution)/shard_map/psum | solution.py:12
  736.9 40.3 %while.162 = (s32[]{:T(128)}, s32[128,128]{1,0:T(8,128)S(1)}, s32[]{:T(128)}) while((s32[]{:T(128)}, s32[128,128]{1,0:T(8,128)S(1)}, s32[]{:T(128)}) %tuple.299), condition=%wide.region_22.23_spmd, body=%wide.region_21.22_spmd.sunk | while | flops 32770 | bytes 134197 | solution.py:36
  777.2 50.6 %while.163 = (s32[]{:T(128)}, s32[512,128]{1,0:T(8,128)S(1)}, s32[512,128]{1,0:T(8,128)S(1)}, s32[128,128]{1,0:T(8,128)S(1)}, s32[]{:T(128)}, /*index=5*/s32[]{:T(128)}, s32[]{:T(128)}, s32[]{:T(128)}) while((s32[]{:T(128)}, s32[512,128]{1,0:T(8,128)S(1)}, s32[512,128]{1,0:T(8,128)S(1)}, s32[128,128]{1,0:T(8,128)S(1)}, s32[]{:T(128)}, ...), condition=%wide.region_25.26_spmd, body=%wide.region_23.25_spmd.sunk | while | flops 1048582 | bytes 1110155 | solution.py:25
  828.9 34.6 %all-reduce.19.cloned.1.call-done = s32[512,128]{1,0:T(8,128)} async-done(((s32[512,128]{1,0:T(8,128)}), s32[512,128]{1,0:T(8,128)}) %all-reduce.19.cloned.1.call-update) | async-done | bytes 262160 | tf_op jit(solution)/shard_map/psum | solution.py:12
  863.5 150.9 %while.164 = (s32[]{:T(128)}, s32[512,1024]{1,0:T(8,128)S(1)}, s32[512,128]{1,0:T(8,128)}, s32[128,1024]{1,0:T(8,128)}, s32[]{:T(128)}, /*index=5*/s32[]{:T(128)}, s32[]{:T(128)}, s32[]{:T(128)}) while((s32[]{:T(128)}, s32[512,1024]{1,0:T(8,128)S(1)}, s32[512,128]{1,0:T(8,128)}, s32[128,1024]{1,0:T(8,128)}, s32[]{:T(128)}, ...), condition=%wide.region_29.30_spmd, body=%wide.region_27.29_spmd.sunk | while | flops 8388614 | bytes 8536203 | solution.py:25
  1015.4 54.7 %all-reduce.21.cloned.1.call-done = s32[128,1024]{1,0:T(8,128)} async-done(((s32[128,1024]{1,0:T(8,128)}), s32[128,1024]{1,0:T(8,128)}) %all-reduce.21.cloned.1.call-update) | async-done | bytes 524304 | tf_op jit(solution)/shard_map/psum | solution.py:12
  1071.0 40.3 %while.165 = (s32[]{:T(128)}, s32[128,128]{1,0:T(8,128)S(1)}, s32[]{:T(128)}) while((s32[]{:T(128)}, s32[128,128]{1,0:T(8,128)S(1)}, s32[]{:T(128)}) %tuple.308), condition=%wide.region_32.33_spmd, body=%wide.region_31.32_spmd.sunk | while | flops 32770 | bytes 134197 | solution.py:36
  1111.3 50.6 %while.166 = (s32[]{:T(128)}, s32[512,128]{1,0:T(8,128)S(1)}, s32[512,128]{1,0:T(8,128)S(1)}, s32[128,128]{1,0:T(8,128)S(1)}, s32[]{:T(128)}, /*index=5*/s32[]{:T(128)}, s32[]{:T(128)}, s32[]{:T(128)}) while((s32[]{:T(128)}, s32[512,128]{1,0:T(8,128)S(1)}, s32[512,128]{1,0:T(8,128)S(1)}, s32[128,128]{1,0:T(8,128)S(1)}, s32[]{:T(128)}, ...), condition=%wide.region_35.36_spmd, body=%wide.region_33.35_spmd.sunk | while | flops 1048582 | bytes 1110155 | solution.py:25
  1162.7 34.9 %all-reduce.23.cloned.1.call-done = s32[512,128]{1,0:T(8,128)} async-done(((s32[512,128]{1,0:T(8,128)}), s32[512,128]{1,0:T(8,128)}) %all-reduce.23.cloned.1.call-update) | async-done | bytes 262160 | tf_op jit(solution)/shard_map/psum | solution.py:12
  1197.5 150.9 %while.167 = (s32[]{:T(128)}, s32[512,1024]{1,0:T(8,128)S(1)}, s32[512,128]{1,0:T(8,128)}, s32[128,1024]{1,0:T(8,128)}, s32[]{:T(128)}, /*index=5*/s32[]{:T(128)}, s32[]{:T(128)}, s32[]{:T(128)}) while((s32[]{:T(128)}, s32[512,1024]{1,0:T(8,128)S(1)}, s32[512,128]{1,0:T(8,128)}, s32[128,1024]{1,0:T(8,128)}, s32[]{:T(128)}, ...), condition=%wide.region_39.40_spmd, body=%wide.region_37.39_spmd.sunk | while | flops 8388614 | bytes 8536203 | solution.py:25
  (2085 shorter events, 929.5 us)
Async XLA Ops:
  6.5 61.4 %all-reduce.9.cloned.1.call-start = ((), (), s32[]{:S(2)}) async-start(), calls=%async_computation | async-start | bytes 1048576 | tf_op jit(solution)/shard_map/psum | solution.py:12
  9.2 186.2 %all-reduce.11.cloned.1.call-start = ((), (), s32[]{:S(2)}) async-start(), calls=%async_computation.1 | async-start | bytes 524288 | tf_op jit(solution)/shard_map/psum | solution.py:12
  160.5 241.5 %all-reduce.13.cloned.1.call-start = ((), (), s32[]{:S(2)}) async-start(), calls=%async_computation.2 | async-start | bytes 1048576 | tf_op jit(solution)/shard_map/psum | solution.py:12
  347.2 182.3 %all-reduce.15.cloned.1.call-start = ((), (), s32[]{:S(2)}) async-start(), calls=%async_computation.3 | async-start | bytes 524288 | tf_op jit(solution)/shard_map/psum | solution.py:12
  494.6 241.5 %all-reduce.17.cloned.1.call-start = ((), (), s32[]{:S(2)}) async-start(), calls=%async_computation.4 | async-start | bytes 1048576 | tf_op jit(solution)/shard_map/psum | solution.py:12
  681.2 182.3 %all-reduce.19.cloned.1.call-start = ((), (), s32[]{:S(2)}) async-start(), calls=%async_computation.5 | async-start | bytes 524288 | tf_op jit(solution)/shard_map/psum | solution.py:12
  828.6 241.5 %all-reduce.21.cloned.1.call-start = ((), (), s32[]{:S(2)}) async-start(), calls=%async_computation.6 | async-start | bytes 1048576 | tf_op jit(solution)/shard_map/psum | solution.py:12
  1015.3 182.3 %all-reduce.23.cloned.1.call-start = ((), (), s32[]{:S(2)}) async-start(), calls=%async_computation.7 | async-start | bytes 524288 | tf_op jit(solution)/shard_map/psum | solution.py:12
  1348.4 1.3 copy-start
Sparse Core Ops, SparseCore 0:
  10.4 57.5 all-reduce.8
  160.7 34.7 all-reduce.10
  347.3 54.6 all-reduce.12
  494.7 34.7 all-reduce.14
  681.3 54.6 all-reduce.16
  828.8 34.7 all-reduce.18
  1015.4 54.6 all-reduce.20
  1162.8 34.7 all-reduce.22
where the time goes:
time: 1360 us
  other arithmetic  730 us (54%)
  waiting for transfers between devices  362 us (27%)
  local copies, waits for them, and re-layouts  226 us (17%)
  loops' own time  23.8 us (2%)
  between operations  13.7 us (1%)
    reduce_min x128, other arithmetic, update(): jnp.min(left_part[:, :, None] + right_part[None, :, :], axis=1)  628 us
    psum x8, waiting for transfers between devices, broadcast(): return lax.psum(kept, axis)  362 us
    dynamic_slice x512, local copies, waits for them, and re-layouts, relax(): column = lax.dynamic_slice_in_dim(current, vertex, 1, 1)  89.7 us
    dynamic_slice x128, local copies, waits for them, and re-layouts, update(): left_part = lax.dynamic_slice_in_dim(left, begin, group, 1)  77 us
    dynamic_slice x128, local copies, waits for them, and re-layouts, update(): right_part = lax.dynamic_slice_in_dim(right, begin, group, 0)  49.8 us
    min x512, other arithmetic, relax(): return jnp.minimum(current, column + across)  49 us
    min x128, other arithmetic, update(): jnp.minimum(total, jnp.min(left_part[:, :, None] + right_part[None, :, :]...  45.4 us
  transfers between devices with their start and end apart: 8, of which 8 were waited for; matrix products, arithmetic and copies ran while one was open for 0% of the time, Pallas kernels for 0%

commit v1 on v0

--- a/solution.py
+++ b/solution.py
@@ -9,7 +9,7 @@
 
 def broadcast(value, axis, source):
     kept = jnp.where(lax.axis_index(axis) == source, value, 0).astype(value.dtype)
-    return lax.psum(kept, axis)
+    return jnp.sum(lax.all_gather(kept, axis), axis=0)
 
 
 def min_plus(acc, left, right):

time: 1360 us -> 1160 us (0.85)
  local copies, waits for them, and re-layouts: 226 us -> 114 us
  waiting for transfers between devices: 362 us -> 260 us
  other arithmetic: 730 us -> 746 us
    psum x8 -> x0, waiting for transfers between devices: 362 us -> none  [broadcast(): return lax.psum(kept, axis)]
    all_gather x0 -> x8, waiting for transfers between devices: none -> 259 us  [broadcast(): return jnp.sum(lax.all_gather(kept, axis), axis=0)]
    dynamic_slice x128, local copies, waits for them, and re-layouts: 77 us -> 16.1 us  [update(): left_part = lax.dynamic_slice_in_dim(left, begin, group, 1)]
    dynamic_slice x128, local copies, waits for them, and re-layouts: 49.8 us -> 1.45 us  [update(): right_part = lax.dynamic_slice_in_dim(right, begin, group, 0)]
    reduce_sum x0 -> x8, other arithmetic: none -> 15.7 us  [broadcast(): return jnp.sum(lax.all_gather(kept, axis), axis=0)]
where the time goes in v1:
time: 1160 us
  other arithmetic  746 us (64%)
  waiting for transfers between devices  260 us (22%)
  local copies, waits for them, and re-layouts  114 us (10%)
  loops' own time  24.4 us (2%)
  between operations  13.8 us (1%)
    reduce_min x128, other arithmetic, update(): jnp.min(left_part[:, :, None] + right_part[None, :, :], axis=1)  628 us
    all_gather x8, waiting for transfers between devices, broadcast(): return jnp.sum(lax.all_gather(kept, axis), axis=0)  259 us
    dynamic_slice x512, local copies, waits for them, and re-layouts, relax(): column = lax.dynamic_slice_in_dim(current, vertex, 1, 1)  89.7 us
    min x512, other arithmetic, relax(): return jnp.minimum(current, column + across)  49 us
    min x128, other arithmetic, update(): jnp.minimum(total, jnp.min(left_part[:, :, None] + right_part[None, :, :]...  45.4 us
  transfers between devices with their start and end apart: 8, of which 8 were waited for; matrix products, arithmetic and copies ran while one was open for 0% of the time, Pallas kernels for 0%

profile of v1, /device:TPU:0, one launch (start us, length us, event | category | flops | bytes accessed | tf_op | source)
XLA Modules:
  0.0 1158.2 jit_solution(3867862979090990905)
XLA Ops:
  9.3 39.3 %all-gather.17.cloned.1.call-done = s32[1024,1024]{1,0:T(8,128)} async-done(((s32[128,1024]{1,0:T(8,128)}), s32[1024,1024]{1,0:T(8,128)}) %all-gather.17.cloned.1.call-update) | async-done | bytes 4194320 | tf_op jit(solution)/shard_map/all_gather | solution.py:12
  51.3 40.4 %while.156 = (s32[]{:T(128)}, s32[128,128]{1,0:T(8,128)S(1)}, s32[]{:T(128)}) while((s32[]{:T(128)}, s32[128,128]{1,0:T(8,128)S(1)}, s32[]{:T(128)}) %tuple.281), condition=%wide.region_2.3_spmd, body=%wide.region_1.2_spmd.sunk | while | flops 32770 | bytes 134197 | solution.py:36
  91.7 50.6 %while.157 = (s32[]{:T(128)}, s32[512,128]{1,0:T(8,128)S(1)}, s32[512,128]{1,0:T(8,128)S(1)}, s32[128,128]{1,0:T(8,128)S(1)}, s32[]{:T(128)}, /*index=5*/s32[]{:T(128)}, s32[]{:T(128)}, s32[]{:T(128)}) while((s32[]{:T(128)}, s32[512,128]{1,0:T(8,128)S(1)}, s32[512,128]{1,0:T(8,128)S(1)}, s32[128,128]{1,0:T(8,128)S(1)}, s32[]{:T(128)}, ...), condition=%wide.region_5.6_spmd, body=%wide.region_3.5_spmd.sunk | while | flops 1048582 | bytes 1110155 | solution.py:25
  143.1 28.1 %all-gather.19.cloned.1.call-done = s32[2048,128]{1,0:T(8,128)} async-done(((s32[512,128]{1,0:T(8,128)}), s32[2048,128]{1,0:T(8,128)}) %all-gather.19.cloned.1.call-update) | async-done | bytes 1048592 | tf_op jit(solution)/shard_map/all_gather | solution.py:12
  172.5 123.8 %while.158 = (s32[]{:T(128)}, s32[512,1024]{1,0:T(8,128)S(1)}, s32[512,128]{1,0:T(8,128)S(1)}, s32[128,1024]{1,0:T(8,128)S(1)}, s32[]{:T(128)}, /*index=5*/s32[]{:T(128)}, s32[]{:T(128)}, s32[]{:T(128)}) while((s32[]{:T(128)}, s32[512,1024]{1,0:T(8,128)S(1)}, s32[512,128]{1,0:T(8,128)S(1)}, s32[128,1024]{1,0:T(8,128)S(1)}, s32[]{:T(128)}, ...), condition=%wide.region_9.10_spmd, body=%wide.region_7.9_spmd.sunk | while | flops 8388614 | bytes 8536203 | solution.py:25
  180.4 6.9 add_reduce_fusion.17
  188.1 6.9 add_reduce_fusion.17
  195.9 6.9 add_reduce_fusion.17
  203.6 6.9 add_reduce_fusion.17
  297.3 36.0 %all-gather.21.cloned.1.call-done = s32[1024,1024]{1,0:T(8,128)} async-done(((s32[128,1024]{1,0:T(8,128)}), s32[1024,1024]{1,0:T(8,128)}) %all-gather.21.cloned.1.call-update) | async-done | bytes 4194320 | tf_op jit(solution)/shard_map/all_gather | solution.py:12
  335.9 40.4 %while.159 = (s32[]{:T(128)}, s32[128,128]{1,0:T(8,128)S(1)}, s32[]{:T(128)}) while((s32[]{:T(128)}, s32[128,128]{1,0:T(8,128)S(1)}, s32[]{:T(128)}) %tuple.290), condition=%wide.region_12.13_spmd, body=%wide.region_11.12_spmd.sunk | while | flops 32770 | bytes 134197 | solution.py:36
  376.3 50.6 %while.160 = (s32[]{:T(128)}, s32[512,128]{1,0:T(8,128)S(1)}, s32[512,128]{1,0:T(8,128)S(1)}, s32[128,128]{1,0:T(8,128)S(1)}, s32[]{:T(128)}, /*index=5*/s32[]{:T(128)}, s32[]{:T(128)}, s32[]{:T(128)}) while((s32[]{:T(128)}, s32[512,128]{1,0:T(8,128)S(1)}, s32[512,128]{1,0:T(8,128)S(1)}, s32[128,128]{1,0:T(8,128)S(1)}, s32[]{:T(128)}, ...), condition=%wide.region_15.16_spmd, body=%wide.region_13.15_spmd.sunk | while | flops 1048582 | bytes 1110155 | solution.py:25
  427.7 28.1 %all-gather.23.cloned.1.call-done = s32[2048,128]{1,0:T(8,128)} async-done(((s32[512,128]{1,0:T(8,128)}), s32[2048,128]{1,0:T(8,128)}) %all-gather.23.cloned.1.call-update) | async-done | bytes 1048592 | tf_op jit(solution)/shard_map/all_gather | solution.py:12
  457.1 123.8 %while.161 = (s32[]{:T(128)}, s32[512,1024]{1,0:T(8,128)S(1)}, s32[512,128]{1,0:T(8,128)S(1)}, s32[128,1024]{1,0:T(8,128)S(1)}, s32[]{:T(128)}, /*index=5*/s32[]{:T(128)}, s32[]{:T(128)}, s32[]{:T(128)}) while((s32[]{:T(128)}, s32[512,1024]{1,0:T(8,128)S(1)}, s32[512,128]{1,0:T(8,128)S(1)}, s32[128,1024]{1,0:T(8,128)S(1)}, s32[]{:T(128)}, ...), condition=%wide.region_19.20_spmd, body=%wide.region_17.19_spmd.sunk | while | flops 8388614 | bytes 8536203 | solution.py:25
  582.1 35.8 %all-gather.25.cloned.1.call-done = s32[1024,1024]{1,0:T(8,128)} async-done(((s32[128,1024]{1,0:T(8,128)}), s32[1024,1024]{1,0:T(8,128)}) %all-gather.25.cloned.1.call-update) | async-done | bytes 4194320 | tf_op jit(solution)/shard_map/all_gather | solution.py:12
  620.5 40.4 %while.162 = (s32[]{:T(128)}, s32[128,128]{1,0:T(8,128)S(1)}, s32[]{:T(128)}) while((s32[]{:T(128)}, s32[128,128]{1,0:T(8,128)S(1)}, s32[]{:T(128)}) %tuple.299), condition=%wide.region_22.23_spmd, body=%wide.region_21.22_spmd.sunk | while | flops 32770 | bytes 134197 | solution.py:36
  660.9 50.6 %while.163 = (s32[]{:T(128)}, s32[512,128]{1,0:T(8,128)S(1)}, s32[512,128]{1,0:T(8,128)S(1)}, s32[128,128]{1,0:T(8,128)S(1)}, s32[]{:T(128)}, /*index=5*/s32[]{:T(128)}, s32[]{:T(128)}, s32[]{:T(128)}) while((s32[]{:T(128)}, s32[512,128]{1,0:T(8,128)S(1)}, s32[512,128]{1,0:T(8,128)S(1)}, s32[128,128]{1,0:T(8,128)S(1)}, s32[]{:T(128)}, ...), condition=%wide.region_25.26_spmd, body=%wide.region_23.25_spmd.sunk | while | flops 1048582 | bytes 1110155 | solution.py:25
  712.3 28.1 %all-gather.27.cloned.1.call-done = s32[2048,128]{1,0:T(8,128)} async-done(((s32[512,128]{1,0:T(8,128)}), s32[2048,128]{1,0:T(8,128)}) %all-gather.27.cloned.1.call-update) | async-done | bytes 1048592 | tf_op jit(solution)/shard_map/all_gather | solution.py:12
  741.7 123.8 %while.164 = (s32[]{:T(128)}, s32[512,1024]{1,0:T(8,128)S(1)}, s32[512,128]{1,0:T(8,128)S(1)}, s32[128,1024]{1,0:T(8,128)S(1)}, s32[]{:T(128)}, /*index=5*/s32[]{:T(128)}, s32[]{:T(128)}, s32[]{:T(128)}) while((s32[]{:T(128)}, s32[512,1024]{1,0:T(8,128)S(1)}, s32[512,128]{1,0:T(8,128)S(1)}, s32[128,1024]{1,0:T(8,128)S(1)}, s32[]{:T(128)}, ...), condition=%wide.region_29.30_spmd, body=%wide.region_27.29_spmd.sunk | while | flops 8388614 | bytes 8536203 | solution.py:25
  866.5 36.0 %all-gather.29.cloned.1.call-done = s32[1024,1024]{1,0:T(8,128)} async-done(((s32[128,1024]{1,0:T(8,128)}), s32[1024,1024]{1,0:T(8,128)}) %all-gather.29.cloned.1.call-update) | async-done | bytes 4194320 | tf_op jit(solution)/shard_map/all_gather | solution.py:12
  905.1 40.4 %while.165 = (s32[]{:T(128)}, s32[128,128]{1,0:T(8,128)S(1)}, s32[]{:T(128)}) while((s32[]{:T(128)}, s32[128,128]{1,0:T(8,128)S(1)}, s32[]{:T(128)}) %tuple.308), condition=%wide.region_32.33_spmd, body=%wide.region_31.32_spmd.sunk | while | flops 32770 | bytes 134197 | solution.py:36
  945.5 50.6 %while.166 = (s32[]{:T(128)}, s32[512,128]{1,0:T(8,128)S(1)}, s32[512,128]{1,0:T(8,128)S(1)}, s32[128,128]{1,0:T(8,128)S(1)}, s32[]{:T(128)}, /*index=5*/s32[]{:T(128)}, s32[]{:T(128)}, s32[]{:T(128)}) while((s32[]{:T(128)}, s32[512,128]{1,0:T(8,128)S(1)}, s32[512,128]{1,0:T(8,128)S(1)}, s32[128,128]{1,0:T(8,128)S(1)}, s32[]{:T(128)}, ...), condition=%wide.region_35.36_spmd, body=%wide.region_33.35_spmd.sunk | while | flops 1048582 | bytes 1110155 | solution.py:25
  996.8 28.1 %all-gather.31.cloned.1.call-done = s32[2048,128]{1,0:T(8,128)} async-done(((s32[512,128]{1,0:T(8,128)}), s32[2048,128]{1,0:T(8,128)}) %all-gather.31.cloned.1.call-update) | async-done | bytes 1048592 | tf_op jit(solution)/shard_map/all_gather | solution.py:12
  1026.3 123.8 %while.167 = (s32[]{:T(128)}, s32[512,1024]{1,0:T(8,128)S(1)}, s32[512,128]{1,0:T(8,128)S(1)}, s32[128,1024]{1,0:T(8,128)S(1)}, s32[]{:T(128)}, /*index=5*/s32[]{:T(128)}, s32[]{:T(128)}, s32[]{:T(128)}) while((s32[]{:T(128)}, s32[512,1024]{1,0:T(8,128)S(1)}, s32[512,128]{1,0:T(8,128)S(1)}, s32[128,1024]{1,0:T(8,128)S(1)}, s32[]{:T(128)}, ...), condition=%wide.region_39.40_spmd, body=%wide.region_37.39_spmd.sunk | while | flops 8388614 | bytes 8536203 | solution.py:25
  (2093 shorter events, 832.9 us)
Async XLA Ops:
  6.5 42.1 %all-gather.17.cloned.1.call-start = ((), (), s32[]{:S(2)}) async-start(), calls=%async_computation | async-start | bytes 4718592 | tf_op jit(solution)/shard_map/all_gather | solution.py:12
  9.2 162.0 %all-gather.19.cloned.1.call-start = ((), (), s32[]{:S(2)}) async-start(), calls=%async_computation.1 | async-start | bytes 1310720 | tf_op jit(solution)/shard_map/all_gather | solution.py:12
  143.1 190.2 %all-gather.21.cloned.1.call-start = ((), (), s32[]{:S(2)}) async-start(), calls=%async_computation.2 | async-start | bytes 4718592 | tf_op jit(solution)/shard_map/all_gather | solution.py:12
  297.2 158.6 %all-gather.23.cloned.1.call-start = ((), (), s32[]{:S(2)}) async-start(), calls=%async_computation.3 | async-start | bytes 1310720 | tf_op jit(solution)/shard_map/all_gather | solution.py:12
  427.7 190.2 %all-gather.25.cloned.1.call-start = ((), (), s32[]{:S(2)}) async-start(), calls=%async_computation.4 | async-start | bytes 4718592 | tf_op jit(solution)/shard_map/all_gather | solution.py:12
  581.8 158.6 %all-gather.27.cloned.1.call-start = ((), (), s32[]{:S(2)}) async-start(), calls=%async_computation.5 | async-start | bytes 1310720 | tf_op jit(solution)/shard_map/all_gather | solution.py:12
  712.2 190.2 %all-gather.29.cloned.1.call-start = ((), (), s32[]{:S(2)}) async-start(), calls=%async_computation.6 | async-start | bytes 4718592 | tf_op jit(solution)/shard_map/all_gather | solution.py:12
  866.4 158.6 %all-gather.31.cloned.1.call-start = ((), (), s32[]{:S(2)}) async-start(), calls=%async_computation.7 | async-start | bytes 1310720 | tf_op jit(solution)/shard_map/all_gather | solution.py:12
  1150.1 1.3 copy-start
Sparse Core Ops, SparseCore 0:
  9.3 39.2 all-gather.16
  143.2 27.9 all-gather.18
  297.3 35.9 all-gather.20
  427.8 27.9 all-gather.22
  581.9 35.9 all-gather.24
  712.4 27.9 all-gather.26
  866.5 35.9 all-gather.28
  997.0 27.9 all-gather.30
